TPU v7x, 32 devices: a whole 2x2x4 slice. The times are simulated.
32 devices in a mesh: expert: 4 (over z), shard: 8 (over y, x, core).
Axes of the slice: x: 2, y: 2, z: 4, core: 2. Of those that a mesh axis runs over, the one named last changes fastest.
Arguments:
- master_gate: float32 [64, 2048, 1024], P('expert', 'shard'), may hold values from -0.1875 to 0.1875
- second_gate: float32 [64, 2048, 1024], P('expert', 'shard'), may hold values from -0.125 to 0.125
- master_up: float32 [64, 2048, 1024], P('expert', 'shard'), may hold values from -0.1875 to 0.1875
- second_up: float32 [64, 2048, 1024], P('expert', 'shard'), may hold values from -0.125 to 0.125
- mix_share: float32 [64], P('expert'), may hold values from 0.2 to 0.8
- router_weight: float32 [2048, 64], P('shard', 'expert'), may hold values from -0.125 to 0.125
- router_gain: float32 [2048], P('shard'), may hold values from 0.25 to 1.75
Outputs:
- final_gate: bfloat16 [64, 2048, 1024], P('expert', None, 'shard')
- final_up: bfloat16 [64, 2048, 1024], P('expert', None, 'shard')
- scale_gate: float32 [64, 1024], P('expert', 'shard')
- scale_up: float32 [64, 1024], P('expert', 'shard')
- serve_router: bfloat16 [2048, 64], replicated
All inputs are finite; a program needn't handle non-finite values.
Results may differ from a plain program's by a relative error of at most 0.001.
Values may be sent and summed in bfloat16 or wider, within the bound.
A program may use at most 256 MiB of HBM per device.

v0:
```python
import jax
import jax.numpy as jnp
from jax import lax
from jax.sharding import PartitionSpec as P

D_MODEL = 2048


def local(master_gate, second_gate, master_up, second_up, mix_share, router_weight, router_gain):
    merged_gate = (
        mix_share[:, None, None] * master_gate + (1.0 - mix_share[:, None, None]) * second_gate
    )
    merged_up = mix_share[:, None, None] * master_up + (1.0 - mix_share[:, None, None]) * second_up
    total_gate, total_up = lax.psum(
        (jnp.sum(jnp.abs(merged_gate), axis=1), jnp.sum(jnp.abs(merged_up), axis=1)), "shard"
    )
    scale_gate = total_gate / D_MODEL
    scale_up = total_up / D_MODEL
    narrow_gate, narrow_up = (
        (merged_gate / jnp.expand_dims(scale_gate, 1)).astype(jnp.bfloat16),
        (merged_up / jnp.expand_dims(scale_up, 1)).astype(jnp.bfloat16),
    )
    final_gate, final_up = (
        lax.all_to_all(narrow_gate, "shard", split_axis=2, concat_axis=1, tiled=True),
        lax.all_to_all(narrow_up, "shard", split_axis=2, concat_axis=1, tiled=True),
    )
    scale_gate = lax.dynamic_slice_in_dim(
        scale_gate, lax.axis_index("shard") * final_gate.shape[2], final_gate.shape[2], axis=1
    )
    scale_up = lax.dynamic_slice_in_dim(
        scale_up, lax.axis_index("shard") * final_up.shape[2], final_up.shape[2], axis=1
    )
    part_router = (router_weight * router_gain[:, None]).astype(jnp.bfloat16)
    row_router = lax.all_gather(part_router, "shard", axis=0, tiled=True)
    serve_router = lax.all_gather(row_router, "expert", axis=1, tiled=True)
    return (final_gate, final_up, scale_gate, scale_up, serve_router)


def solution(mesh):
    placed = (
        P("expert", "shard", None),
        P("expert", "shard", None),
        P("expert", "shard", None),
        P("expert", "shard", None),
        P("expert"),
        P("shard", "expert"),
        P("shard"),
    )
    return jax.shard_map(
        local,
        mesh=mesh,
        in_specs=placed,
        out_specs=(
            P("expert", None, "shard"),
            P("expert", None, "shard"),
            P("expert", "shard"),
            P("expert", "shard"),
            P(),
        ),
        check_vma=False,
    )
```

profile of v0, /device:TPU:0, one launch (start us, length us, event | category | flops | bytes accessed | tf_op | source)
XLA Modules:
  0.0 434.8 jit_solution(18230987575285412976)
XLA Ops:
  7.2 0.0 all-reduce.3.cloned.1.call-start
  7.2 17.6 %copy.22 = f32[16,256,1024]{1,0,2:T(8,128)} copy(f32[16,256,1024]{2,1,0:T(8,128)} %param.7) | data formatting | bytes 33554432 | tf_op args[0]
  24.8 17.6 %copy.23 = f32[16,256,1024]{1,0,2:T(8,128)} copy(f32[16,256,1024]{2,1,0:T(8,128)} %param.8) | data formatting | bytes 33554432 | tf_op args[1]
  42.4 17.6 %copy.25 = f32[16,256,1024]{1,0,2:T(8,128)} copy(f32[16,256,1024]{2,1,0:T(8,128)} %param.9) | data formatting | bytes 33554432 | tf_op args[2]
  60.0 0.0 copy-start.1
  60.0 17.6 %copy.26 = f32[16,256,1024]{1,0,2:T(8,128)} copy(f32[16,256,1024]{2,1,0:T(8,128)} %param.10) | data formatting | bytes 33554432 | tf_op args[3]
  77.6 0.0 copy-done.1
  77.6 23.7 %abs_reduce_fusion = (f32[16,1024]{0,1:T(8,128)}, f32[16,1024]{0,1:T(8,128)}) fusion(f32[16,256,1024]{1,0,2:T(8,128)} %copy.26, f32[16]{0:T(128)S(1)} %broadcast_subtract_fusion, f32[16,256,1024]{1,0,2:T(8,128)} %copy.25, f32[16]{0:T(128)S(1)} %copy-done.1, f32[16,256,1024]{1,0,2:T(8,128)} %copy.23, f32[16,256,1024]{1,0,2:T(8,128)} %copy.22), kind=kLoop, calls=%fused_computation.1 | loop fusion | flops 41910272 | bytes 67240064 | tf_op jit(solution)/shard_map/reduce_sum | solution.py:15
  101.3 0.0 all-reduce.3.cloned.1.call-update
  101.4 59.6 %all-reduce.3.cloned.1.call-done = (f32[16,1024]{0,1:T(8,128)}, f32[16,1024]{0,1:T(8,128)}) async-done(((f32[16,1024]{0,1:T(8,128)}, f32[16,1024]{0,1:T(8,128)}), (f32[16,1024]{0,1:T(8,128)}, f32[16,1024]{0,1:T(8,128)})) %all-reduce.3.cloned.1.call-update) | async-done | bytes 131088 | tf_op jit(solution)/shard_map/psum | solution.py:14
  161.0 1.3 broadcast_multiply_fusion
  162.3 25.3 %divide_convert_fusion = (bf16[16,256,1024]{1,0,2:T(8,128)(2,1)}, bf16[16,256,1024]{1,0,2:T(8,128)(2,1)S(1)}) fusion(f32[16,1024]{0,1:T(8,128)S(1)} %get-tuple-element.16, f32[16,256,1024]{1,0,2:T(8,128)} %copy.26, f32[16]{0:T(128)S(1)} %broadcast_subtract_fusion, f32[16,256,1024]{1,0,2:T(8,128)} %copy.25, f32[16]{0:T(128)S(1)} %copy-done.1, ...), kind=kLoop, calls=%fused_computation | loop fusion | flops 41943040 | bytes 84017280 | tf_op jit(solution)/shard_map/convert_element_type | solution.py:21
  187.6 97.6 %all_to_all.36 = bf16[16,256,1024]{1,0,2:T(8,128)(2,1)} all-to-all(bf16[16,256,1024]{1,0,2:T(8,128)(2,1)S(1)} %get-tuple-element.15), channel_id=1, replica_groups=mesh['expert'=4,'shard'=8] {'shard'}, dimensions={2} | all-to-all | bytes 16777216 | tf_op jit(solution)/shard_map/all_to_all | solution.py:24
  285.2 4.9 %all-to-all-start.1 = ((bf16[16,256,1024]{1,0,2:T(8,128)(2,1)}), bf16[16,256,1024]{1,0,2:T(8,128)(2,1)}, u32[]{:S(2)}, u32[]{:S(2)}) async-start(bf16[16,256,1024]{1,0,2:T(8,128)(2,1)} %get-tuple-element.14), calls=%async_computation.1 | async-start | bytes 16777216 | tf_op jit(solution)/shard_map/all_to_all | solution.py:25
  290.2 0.0 copy-done
  290.2 0.0 copy-done.2
  290.2 97.2 %all_gather.6 = bf16[2048,16]{0,1:T(8,128)(2,1)S(1)} all-gather(bf16[256,16]{0,1:T(8,128)(2,1)S(1)} %multiply_convert_fusion), channel_id=1, replica_groups=mesh['expert'=4,'shard'=8] {'shard'}, dimensions={0}, use_global_device_ids=true | all-gather | bytes 73728 | tf_op jit(solution)/shard_map/all_gather | solution.py:34
  387.4 14.0 %all_gather.7 = bf16[2048,64]{0,1:T(8,128)(2,1)S(1)} all-gather(bf16[2048,16]{0,1:T(8,128)(2,1)S(1)} %all_gather.6), channel_id=1, replica_groups=mesh['expert'=4,'shard'=8] {'expert'}, dimensions={1}, use_global_device_ids=true | all-gather | bytes 327680 | tf_op jit(solution)/shard_map/all_gather | solution.py:35
  401.3 0.7 copy.28
  402.0 0.7 copy.29
  402.7 12.3 %copy.24 = bf16[16,8,256,128]{3,2,1,0:T(8,128)(2,1)} copy(bf16[16,8,256,128]{2,0,3,1:T(8,128)(2,1)} %bitcast.8) | data formatting | bytes 16777216 | tf_op jit(solution)/shard_map/all_to_all | solution.py:24
  415.0 0.0 all-to-all-done.1
  415.0 12.3 %copy.27 = bf16[16,8,256,128]{3,2,1,0:T(8,128)(2,1)} copy(bf16[16,8,256,128]{2,0,3,1:T(8,128)(2,1)} %bitcast.4) | data formatting | bytes 16777216 | tf_op jit(solution)/shard_map/all_to_all | solution.py:25
  427.2 0.7 copy.33
  (6 shorter events, 0.0 us)
Async XLA Ops:
  7.2 153.8 %all-reduce.3.cloned.1.call-start = ((), (), s32[]{:S(2)}) async-start(), calls=%async_computation.2 | async-start | bytes 2097152 | tf_op jit(solution)/shard_map/psum | solution.py:14
  60.0 17.6 %copy-start.1 = (f32[16]{0:T(128)S(1)}, f32[16]{0:T(128)}, u32[]{:S(2)}) copy-start(f32[16]{0:T(128)} %param.11) | copy-start | bytes 196
  187.6 102.6 %copy-start = (f32[256,16]{0,1:T(8,128)S(1)}, f32[256,16]{0,1:T(8,128)}, u32[]{:S(2)}) copy-start(f32[256,16]{0,1:T(8,128)} %param.12) | copy-start | bytes 49156
  187.6 102.6 %copy-start.2 = (f32[256]{0:T(256)S(1)}, f32[256]{0:T(256)}, u32[]{:S(2)}) copy-start(f32[256]{0:T(256)} %param.13) | copy-start | bytes 3076
  285.2 129.8 %all-to-all-start.1 = ((bf16[16,256,1024]{1,0,2:T(8,128)(2,1)}), bf16[16,256,1024]{1,0,2:T(8,128)(2,1)}, u32[]{:S(2)}, u32[]{:S(2)}) async-start(bf16[16,256,1024]{1,0,2:T(8,128)(2,1)} %get-tuple-element.14), calls=%async_computation.1 | async-start | bytes 16777216 | tf_op jit(solution)/shard_map/all_to_all | solution.py:25
Sparse Core Ops, SparseCore 0:
  101.5 59.4 all-reduce.2
where the time goes:
time: 437 us; the launch traced here: 435 us
  blocking collectives  209 us (48%)
  local copies, waits for them, and re-layouts  97 us (22%)
  waiting for transfers between devices  59.7 us (14%)
  other arithmetic  50.3 us (12%)
  between operations  14.1 us (3%)
  starting transfers between devices  4.98 us (1%)
    all_to_all x1, blocking collectives, local(): lax.all_to_all(narrow_gate, 'shard', split_axis=2, concat_axis=1, tiled=T...  97.6 us
    all_gather x1, blocking collectives, local(): row_router = lax.all_gather(part_router, 'shard', axis=0, tiled=True)  97.2 us
    unnamed x13, local copies, waits for them, and re-layouts  72.5 us
    psum x1, waiting for transfers between devices, local(): lax.psum((jnp.sum(jnp.abs(merged_gate), axis=1), jnp.sum(jnp.abs(merged_u...  59.6 us
    convert_element_type x1, other arithmetic, local(): (merged_up / jnp.expand_dims(scale_up, 1)).astype(jnp.bfloat16)  25.3 us
    reduce_sum x1, other arithmetic, local(): jnp.sum(jnp.abs(merged_up), axis=1)  23.7 us
    all_gather x1, blocking collectives, local(): serve_router = lax.all_gather(row_router, 'expert', axis=1, tiled=True)  14 us
    all_to_all x1, local copies, waits for them, and re-layouts, local(): lax.all_to_all(narrow_up, 'shard', split_axis=2, concat_axis=1, tiled=True)  12.3 us
  transfers between devices with their start and end apart: 2, of which 1 were waited for; matrix products, arithmetic and copies ran while one was open for 3% of the time, Pallas kernels for 0%

commit v1 on v0

--- a/solution.py
+++ b/solution.py
@@ -4,6 +4,13 @@
 from jax.sharding import PartitionSpec as P
 
 D_MODEL = 2048
+
+
+def stacked_exchange(x, mesh_axis, split, join):
+    count = lax.axis_size(mesh_axis)
+    blocks = jnp.stack(jnp.split(x, count, axis=split), axis=0)
+    blocks = lax.all_to_all(blocks, mesh_axis, split_axis=0, concat_axis=0)
+    return jnp.concatenate(blocks, axis=join)
 
 
 def local(master_gate, second_gate, master_up, second_up, mix_share, router_weight, router_gain):
@@ -21,7 +28,7 @@
         (merged_up / jnp.expand_dims(scale_up, 1)).astype(jnp.bfloat16),
     )
     final_gate, final_up = (
-        lax.all_to_all(narrow_gate, "shard", split_axis=2, concat_axis=1, tiled=True),
+        stacked_exchange(narrow_gate, "shard", 2, 1),
         lax.all_to_all(narrow_up, "shard", split_axis=2, concat_axis=1, tiled=True),
     )
     scale_gate = lax.dynamic_slice_in_dim(

time: 437 us -> 376 us (0.86)
  blocking collectives: 209 us -> 111 us
  waiting for transfers between devices: 59.7 us -> 135 us
  local copies, waits for them, and re-layouts: 97 us -> 49.8 us
  starting transfers between devices: 4.98 us -> 9.99 us
    all_to_all x1 -> x0, blocking collectives: 97.6 us -> none  [local(): lax.all_to_all(narrow_gate, 'shard', split_axis=2, concat_axis=1, tiled=T...]
    all_to_all x1, waiting for transfers between devices: 0.01 us -> 78.9 us  [local(): lax.all_to_all(narrow_up, 'shard', split_axis=2, concat_axis=1, tiled=True)]
    unnamed x13 -> x16, local copies, waits for them, and re-layouts: 72.5 us -> 14.6 us
    convert_element_type x0 -> x1, local copies, waits for them, and re-layouts: none -> 12.6 us  [local(): (merged_up / jnp.expand_dims(scale_up, 1)).astype(jnp.bfloat16)]
    all_to_all x0 -> x1, starting transfers between devices: none -> 5.02 us  [stacked_exchange(): blocks = lax.all_to_all(blocks, mesh_axis, split_axis=0, concat_axis=0)]
    all_to_all x1, local copies, waits for them, and re-layouts: 12.3 us -> 7.89 us  [stacked_exchange(): blocks = lax.all_to_all(blocks, mesh_axis, split_axis=0, concat_axis=0)]
  transfers between devices with their start and end apart: 2 -> 3, of which waited for: 1 -> 2; matrix products, arithmetic and copies ran while one was open for 3% -> 8% of each run, Pallas kernels for 0% -> 0%
where the time goes in v1:
time: 376 us; the launch traced here: 375 us
  waiting for transfers between devices  135 us (36%)
  blocking collectives  111 us (30%)
  other arithmetic  54.3 us (14%)
  local copies, waits for them, and re-layouts  49.8 us (13%)
  between operations  14.1 us (4%)
  starting transfers between devices  9.99 us (3%)
    all_gather x1, blocking collectives, local(): row_router = lax.all_gather(part_router, 'shard', axis=0, tiled=True)  97.2 us
    all_to_all x1, waiting for transfers between devices, local(): lax.all_to_all(narrow_up, 'shard', split_axis=2, concat_axis=1, tiled=True)  78.9 us
    psum x1, waiting for transfers between devices, local(): lax.psum((jnp.sum(jnp.abs(merged_gate), axis=1), jnp.sum(jnp.abs(merged_u...  56.4 us
    convert_element_type x1, other arithmetic, local(): (merged_up / jnp.expand_dims(scale_up, 1)).astype(jnp.bfloat16)  29.4 us
    reduce_sum x1, other arithmetic, local(): jnp.sum(jnp.abs(merged_up), axis=1)  23.3 us
    unnamed x16, local copies, waits for them, and re-layouts  14.6 us
    all_gather x1, blocking collectives, local(): serve_router = lax.all_gather(row_router, 'expert', axis=1, tiled=True)  14 us
    convert_element_type x1, local copies, waits for them, and re-layouts, local(): (merged_up / jnp.expand_dims(scale_up, 1)).astype(jnp.bfloat16)  12.6 us
  transfers between devices with their start and end apart: 3, of which 2 were waited for; matrix products, arithmetic and copies ran while one was open for 8% of the time, Pallas kernels for 0%

profile of v1, /device:TPU:0, one launch (start us, length us, event | category | flops | bytes accessed | tf_op | source)
XLA Modules:
  0.0 374.7 jit_solution(9546674227950947289)
XLA Ops:
  7.2 0.7 broadcast_subtract_fusion
  7.9 23.3 %abs_reduce_fusion = (f32[16,1024]{1,0:T(8,128)}, f32[16,1024]{1,0:T(8,128)}) fusion(f32[16,256,1024]{2,1,0:T(8,128)} %param.10, f32[16]{0:T(128)S(1)} %broadcast_subtract_fusion, f32[16,256,1024]{2,1,0:T(8,128)} %param.9, f32[16]{0:T(128)} %param.11, f32[16,256,1024]{2,1,0:T(8,128)} %param.8, f32[16,256,1024]{2,1,0:T(8,128)} %param.7), kind=kLoop, calls=%fused_computation.1 | loop fusion | flops 41910272 | bytes 67240064 | tf_op jit(solution)/shard_map/reduce_sum | solution.py:22
  31.2 56.4 %all-reduce.3.cloned.1.call-done = (f32[16,1024]{1,0:T(8,128)}, f32[16,1024]{1,0:T(8,128)}) async-done(((f32[16,1024]{1,0:T(8,128)}, f32[16,1024]{1,0:T(8,128)}), (f32[16,1024]{1,0:T(8,128)}, f32[16,1024]{1,0:T(8,128)})) %all-reduce.3.cloned.1.call-update) | async-done | bytes 131088 | tf_op jit(solution)/shard_map/psum | solution.py:21
  87.6 0.9 broadcast_multiply_fusion
  88.5 29.4 %divide_convert_fusion = (bf16[16,256,1024]{2,1,0:T(8,128)(2,1)}, bf16[16,256,1024]{2,1,0:T(8,128)(2,1)}) fusion(f32[16,1024]{1,0:T(8,128)S(1)} %get-tuple-element.11, f32[16,256,1024]{2,1,0:T(8,128)} %param.10, f32[16]{0:T(128)S(1)} %broadcast_subtract_fusion, f32[16,256,1024]{2,1,0:T(8,128)} %param.9, f32[16]{0:T(128)S(1)} %copy-done.2, ...), kind=kLoop, calls=%fused_computation | loop fusion | flops 41943040 | bytes 84017280 | tf_op jit(solution)/shard_map/convert_element_type | solution.py:28
  117.9 12.6 %copy.31 = bf16[16,256,1024]{1,0,2:T(8,128)(2,1)} copy(bf16[16,256,1024]{2,1,0:T(8,128)(2,1)} %get-tuple-element.9) | data formatting | bytes 16777216 | tf_op jit(solution)/shard_map/convert_element_type | solution.py:28
  130.5 4.9 %all-to-all-start.1 = ((bf16[16,256,1024]{1,0,2:T(8,128)(2,1)}), bf16[16,256,1024]{1,0,2:T(8,128)(2,1)}, u32[]{:S(2)}, u32[]{:S(2)}) async-start(bf16[16,256,1024]{1,0,2:T(8,128)(2,1)} %copy.31), calls=%async_computation.1 | async-start | bytes 16777216 | tf_op jit(solution)/shard_map/all_to_all | solution.py:32
  135.5 2.4 fusion.7
  137.9 3.0 fusion.6
  140.9 2.3 fusion.5
  143.2 2.3 fusion.4
  145.5 1.2 fusion.3
  146.8 1.3 fusion.2
  148.1 1.3 fusion.1
  149.3 1.3 fusion
  150.6 78.9 %all-to-all-done.1 = bf16[16,256,1024]{1,0,2:T(8,128)(2,1)} async-done(((bf16[16,256,1024]{1,0,2:T(8,128)(2,1)}), bf16[16,256,1024]{1,0,2:T(8,128)(2,1)}, u32[]{:S(2)}, u32[]{:S(2)}) %all-to-all-start.1) | async-done | bytes 8388640 | tf_op jit(solution)/shard_map/all_to_all | solution.py:32
  229.5 5.0 %all-to-all-start = ((bf16[8,16,256,128]{3,2,1,0:T(8,128)(2,1)}), bf16[8,16,256,128]{3,2,1,0:T(8,128)(2,1)}, u32[]{:S(2)}, u32[]{:S(2)}) async-start(bf16[8,16,256,128]{3,2,1,0:T(8,128)(2,1)} %fusion), calls=%async_computation | async-start | bytes 16777216 | tf_op jit(solution)/shard_map/all_to_all | solution.py:12
  234.6 97.2 %all_gather.6 = bf16[2048,16]{0,1:T(8,128)(2,1)S(1)} all-gather(bf16[256,16]{0,1:T(8,128)(2,1)S(1)} %multiply_convert_fusion), channel_id=1, replica_groups=mesh['expert'=4,'shard'=8] {'shard'}, dimensions={0}, use_global_device_ids=true | all-gather | bytes 73728 | tf_op jit(solution)/shard_map/all_gather | solution.py:41
  331.7 14.0 %all_gather.7 = bf16[2048,64]{0,1:T(8,128)(2,1)S(1)} all-gather(bf16[2048,16]{0,1:T(8,128)(2,1)S(1)} %all_gather.6), channel_id=1, replica_groups=mesh['expert'=4,'shard'=8] {'expert'}, dimensions={1}, use_global_device_ids=true | all-gather | bytes 327680 | tf_op jit(solution)/shard_map/all_gather | solution.py:42
  345.7 0.6 constant_dynamic-slice_fusion
  346.3 0.6 constant_dynamic-slice_fusion.1
  346.9 12.3 %copy.32 = bf16[16,8,256,128]{3,2,1,0:T(8,128)(2,1)} copy(bf16[16,8,256,128]{2,0,3,1:T(8,128)(2,1)} %bitcast.11) | data formatting | bytes 16777216 | tf_op jit(solution)/shard_map/all_to_all | solution.py:32
  359.2 7.9 %copy.30 = bf16[8,16,256,128]{3,2,0,1:T(8,128)(2,1)} copy(bf16[8,16,256,128]{3,2,1,0:T(8,128)(2,1)} %all-to-all-done) | data formatting | bytes 16777216 | tf_op jit(solution)/shard_map/all_to_all | solution.py:12
  367.1 0.7 copy.43
  (12 shorter events, 0.1 us)
Async XLA Ops:
  7.2 80.5 %all-reduce.3.cloned.1.call-start = ((), (), s32[]{:S(2)}) async-start(), calls=%async_computation.2 | async-start | bytes 262144 | tf_op jit(solution)/shard_map/psum | solution.py:21
  7.9 80.7 %copy-start.2 = (f32[16]{0:T(128)S(1)}, f32[16]{0:T(128)}, u32[]{:S(2)}) copy-start(f32[16]{0:T(128)} %param.11) | copy-start | bytes 196
  130.5 99.0 %all-to-all-start.1 = ((bf16[16,256,1024]{1,0,2:T(8,128)(2,1)}), bf16[16,256,1024]{1,0,2:T(8,128)(2,1)}, u32[]{:S(2)}, u32[]{:S(2)}) async-start(bf16[16,256,1024]{1,0,2:T(8,128)(2,1)} %copy.31), calls=%async_computation.1 | async-start | bytes 16777216 | tf_op jit(solution)/shard_map/all_to_all | solution.py:32
  135.5 10.1 %copy-start = (bf16[16,256,1024]{2,1,0:T(8,128)(2,1)S(1)}, bf16[16,256,1024]{2,1,0:T(8,128)(2,1)}, u32[]{:S(2)}) copy-start(bf16[16,256,1024]{2,1,0:T(8,128)(2,1)} %get-tuple-element.10) | copy-start | bytes 25165828
  150.6 83.9 %copy-start.1 = (f32[256,16]{0,1:T(8,128)S(1)}, f32[256,16]{0,1:T(8,128)}, u32[]{:S(2)}) copy-start(f32[256,16]{0,1:T(8,128)} %param.12) | copy-start | bytes 49156
  150.6 83.9 %copy-start.3 = (f32[256]{0:T(256)S(1)}, f32[256]{0:T(256)}, u32[]{:S(2)}) copy-start(f32[256]{0:T(256)} %param.13) | copy-start | bytes 3076
  229.5 129.7 %all-to-all-start = ((bf16[8,16,256,128]{3,2,1,0:T(8,128)(2,1)}), bf16[8,16,256,128]{3,2,1,0:T(8,128)(2,1)}, u32[]{:S(2)}, u32[]{:S(2)}) async-start(bf16[8,16,256,128]{3,2,1,0:T(8,128)(2,1)} %fusion), calls=%async_computation | async-start | bytes 16777216 | tf_op jit(solution)/shard_map/all_to_all | solution.py:12
Sparse Core Ops, SparseCore 0:
  31.3 56.2 all-reduce.2
